TPU v7x, 32 devices: a whole 2x2x4 slice. The times are simulated.
32 devices in a mesh: tensor: 4 (over y, core), context: 8 (over z, x).
Axes of the slice: x: 2, y: 2, z: 4, core: 2. Of those that a mesh axis runs over, the one named last changes fastest.
Arguments:
- query_rows: bfloat16 [2048, 8192], P('context', 'tensor'), may hold values from -160 to 160, as said below
- key_rows: bfloat16 [2048, 1024], P('context'), may hold values from -5 to 5, as said below
- value_rows: bfloat16 [2048, 1024], P('context'), may hold values from -6 to 6
- doc_ids: int32 [2048], P('context'), may hold values from 0 to 3, never falling along the last dimension, each value on 1 to 1024 neighbouring positions
- out_weight: bfloat16 [8192, 8192], P('tensor'), may hold values from -0.09375 to 0.09375
Outputs:
- mixed: bfloat16 [2048, 8192], P('context', 'tensor')
Inputs may be any that keep to these rules, and one draw needn't show every extreme that they name: `query_rows`: within the range given by the table of arrays. `key_rows`: within the range given by the table of arrays. `doc_ids`: document numbers never fall along the sequence; every document has 1 to 1024 tokens and one has exactly 1024.
All inputs are finite; a program needn't handle non-finite values.
Results may differ from a plain program's by a relative error of at most 0.015.
Values may be sent and summed in bfloat16 or wider, within the bound.
No kernel may reach another device: no remote copies, remote signals or barrier semaphores. Data moves between devices by JAX's collectives and lax.ppermute only.
A program may use at most 128 MiB of HBM per device.

v0:
```python
import jax
import jax.numpy as jnp
from jax import lax
from jax.sharding import PartitionSpec as P

H = 64
KVH = 8
HD = 128


NEG_BIG = -1e30


def absorb(running, grouped, query_pos, query_docs, key_block, value_block, doc_block):
    running_max, running_sum, numer = running
    kv_count = grouped.shape[1]
    key_heads = key_block.reshape(key_block.shape[0], kv_count, HD)
    value_heads = value_block.reshape(value_block.shape[0], kv_count, HD)
    key_pos = jnp.arange(key_block.shape[0], dtype=jnp.int32)
    allowed = (
        (key_pos[None, :] <= query_pos[:, None])
        & (doc_block[None, :] == query_docs[:, None])
        & True
    )
    scores = jnp.einsum(
        "tkgd,skd->kgts", grouped, key_heads, preferred_element_type=jnp.float32
    ) * HD ** (-0.5)
    scores = jnp.where(allowed, scores, NEG_BIG)
    fresh_max = jnp.maximum(running_max, jnp.max(scores, axis=-1))
    weights = jnp.where(allowed, jnp.exp(scores - fresh_max[..., None]), 0.0)
    running_sum = jnp.sum(weights, axis=-1)
    numer = jnp.einsum(
        "kgts,skd->kgtd",
        weights.astype(jnp.bfloat16),
        value_heads,
        preferred_element_type=jnp.float32,
    )
    return (fresh_max, running_sum, numer)


def body(query_rows, key_rows, value_rows, doc_ids, out_weight):
    tokens_here = query_rows.shape[0]
    local_heads = query_rows.shape[1] // HD
    group_size = H // KVH
    kv_count = max(1, local_heads // group_size)
    per_kv = local_heads // kv_count
    first_kv = lax.axis_index("tensor") * local_heads // group_size
    key_local = lax.dynamic_slice_in_dim(key_rows, first_kv * HD, kv_count * HD, 1)
    value_local = lax.dynamic_slice_in_dim(value_rows, first_kv * HD, kv_count * HD, 1)
    grouped = query_rows.reshape(tokens_here, kv_count, per_kv, HD)
    block_index = lax.axis_index("context")
    query_pos = block_index * tokens_here + jnp.arange(tokens_here, dtype=jnp.int32)
    initial = (
        jnp.full((kv_count, per_kv, tokens_here), NEG_BIG, jnp.float32),
        jnp.zeros((kv_count, per_kv, tokens_here), jnp.float32),
        jnp.zeros((kv_count, per_kv, tokens_here, HD), jnp.float32),
    )
    running = absorb(
        initial,
        grouped,
        query_pos,
        doc_ids,
        lax.all_gather(key_local, "context", axis=0, tiled=True),
        lax.all_gather(value_local, "context", axis=0, tiled=True),
        lax.all_gather(doc_ids, "context", axis=0, tiled=True),
    )
    final_max, final_sum, numer = running
    attended = numer / final_sum[..., None]
    attended = (
        attended.transpose(2, 0, 1, 3).reshape(tokens_here, local_heads * HD).astype(jnp.bfloat16)
    )
    summed = lax.psum_scatter(
        lax.dot_general(
            out_weight, attended, (((0,), (1,)), ((), ())), preferred_element_type=jnp.float32
        ).astype(jnp.bfloat16),
        "tensor",
        scatter_dimension=0,
        tiled=True,
    ).astype(jnp.float32)
    return summed.T.astype(jnp.bfloat16)


def solution(mesh):
    placed = (
        P("context", "tensor"),
        P("context", None),
        P("context", None),
        P("context"),
        P("tensor", None),
    )
    return jax.shard_map(
        body, mesh=mesh, in_specs=placed, out_specs=P("context", "tensor"), check_vma=False
    )
```

profile of v0, /device:TPU:0, one launch (start us, length us, event | category | flops | bytes accessed | tf_op | source)
XLA Modules:
  0.0 175.1 jit_solution(1525793369700503762)
XLA Ops:
  6.5 0.0 copy-start
  6.5 0.0 all-gather.4.cloned.1.call-start
  6.5 1.0 copy-done
  7.6 0.7 copy.24
  8.3 0.0 all-gather.4.cloned.1.call-update
  8.4 0.0 all-gather.6.cloned.1.call-start
  8.4 1.6 constant_dynamic-slice_fusion
  10.0 0.0 all-gather.6.cloned.1.call-update
  10.0 0.0 reduce-scatter.2.cloned.1.call-start
  10.1 22.6 %all-gather = s32[8,1,256]{2,1,0:T(1,128)S(1)} all-gather(s32[1,1,256]{2,1,0:T(1,128)} %bitcast.48), channel_id=1, replica_groups=mesh['tensor'=4,'context'=8] {'context'}, dimensions={0}, use_global_device_ids=true | all-gather | bytes 9216 | tf_op jit(solution)/shard_map/all_gather | solution.py:65
  32.7 1.4 copy.25
  34.1 1.3 fusion.8
  35.4 16.1 %all-gather.4.cloned.1.call-done = bf16[2048,256]{0,1:T(8,128)(2,1)} async-done(((bf16[256,256]{0,1:T(8,128)(2,1)}), bf16[2048,256]{0,1:T(8,128)(2,1)}) %all-gather.4.cloned.1.call-update) | async-done | bytes 1048592 | tf_op jit(solution)/shard_map/all_gather | solution.py:63
  51.5 15.2 %fusion = (f32[2,8,256]{2,1,0:T(8,128)S(1)}, f32[2,2048,256,8]{2,1,3,0:T(8,128)}) fusion(pred[256,2048]{0,1:T(8,128)(4,1)S(1)} %fusion.8, bf16[2048,2,128,1]{0,2,3,1:T(8,128)(2,1)} %bitcast.45, bf16[256,2,8,128]{3,2,1,0:T(8,128)(2,1)S(1)} %bitcast.41), kind=kOutput, calls=%fused_computation.2 | convolution fusion | flops 2172645376 | bytes 36192256 | tf_op jit(solution)/shard_map/tkgd,skd->kgts/dot_general | solution.py:25
  66.7 14.9 %fusion.1 = f32[2,8,256]{2,1,0:T(8,128)S(1)} fusion(f32[2,2048,256,8]{2,1,3,0:T(8,128)} %get-tuple-element.6, f32[2,8,256]{2,1,0:T(8,128)S(1)} %broadcast_maximum_fusion, pred[256,2048]{0,1:T(8,128)(4,1)S(1)} %fusion.8), kind=kLoop, calls=%fused_computation.3 | loop fusion | flops 41938944 | bytes 34111488 | tf_op jit(solution)/shard_map/reduce_sum | solution.py:31
  81.6 11.4 %all-gather.6.cloned.1.call-done = bf16[2048,256]{1,0:T(8,128)(2,1)} async-done(((bf16[256,256]{1,0:T(8,128)(2,1)}), bf16[2048,256]{1,0:T(8,128)(2,1)}) %all-gather.6.cloned.1.call-update) | async-done | bytes 1048592 | tf_op jit(solution)/shard_map/all_gather | solution.py:64
  93.0 1.5 copy.17
  94.5 0.0 copy-start.1
  94.5 14.1 %fusion.7 = bf16[256,2,8,128]{0,3,2,1:T(8,128)(2,1)S(1)} fusion(bf16[2048,2,128,1]{0,2,3,1:T(8,128)(2,1)S(1)} %bitcast.44, f32[2,2048,256,8]{2,1,3,0:T(8,128)} %get-tuple-element.6, f32[2,8,256]{2,1,0:T(8,128)S(1)} %broadcast_maximum_fusion, pred[256,2048]{0,1:T(8,128)(4,1)S(1)} %fusion.8, f32[256,2,8]{0,2,1:T(8,128)S(1)} %bitcast.47), kind=kOutput, calls=%fused_computation.10 | convolution fusion | flops 2190475264 | bytes 36208640 | tf_op jit(solution)/shard_map/kgts,skd->kgtd/dot_general | solution.py:32
  108.6 16.6 %fusion.6 = bf16[8192,256]{0,1:T(8,128)(2,1)} fusion(bf16[256,2048]{0,1:T(8,128)(2,1)S(1)} %bitcast.42, bf16[2048,8192]{1,0:T(8,128)(2,1)} %param.9), kind=kOutput, calls=%fused_computation.8 | convolution fusion | flops 8592031744 | bytes 38797312 | tf_op jit(solution)/shard_map/dot_general | solution.py:73
  125.2 0.0 reduce-scatter.2.cloned.1.call-update
  125.2 43.3 %reduce-scatter.2.cloned.1.call-done = bf16[2048,256]{0,1:T(8,128)(2,1)} async-done(((bf16[8192,256]{0,1:T(8,128)(2,1)}), bf16[2048,256]{0,1:T(8,128)(2,1)}) %reduce-scatter.2.cloned.1.call-update) | async-done | bytes 1048592 | tf_op jit(solution)/shard_map/reduce_scatter | solution.py:72
  168.5 0.0 copy-done.1
  (3 shorter events, 0.0 us)
Async XLA Ops:
  6.5 1.0 copy-start
  6.5 45.0 %all-gather.4.cloned.1.call-start = ((), (), s32[]{:S(2)}) async-start(), calls=%async_computation.1 | async-start | bytes 1179648 | tf_op jit(solution)/shard_map/all_gather | solution.py:63
  8.4 84.6 %all-gather.6.cloned.1.call-start = ((), (), s32[]{:S(2)}) async-start(), calls=%async_computation.2 | async-start | bytes 1179648 | tf_op jit(solution)/shard_map/all_gather | solution.py:64
  10.0 158.5 %reduce-scatter.2.cloned.1.call-start = ((), (), s32[]{:S(2)}) async-start(), calls=%async_computation.3 | async-start | bytes 5242880 | tf_op jit(solution)/shard_map/reduce_scatter | solution.py:72
  94.5 74.1 %copy-start.1 = (bf16[256,1024]{1,0:T(8,128)(2,1)S(1)}, bf16[256,1024]{1,0:T(8,128)(2,1)}, u32[]{:S(2)}) copy-start(bf16[256,1024]{1,0:T(8,128)(2,1)} %param.6) | copy-start | bytes 1572868
Sparse Core Ops, SparseCore 0:
  9.4 42.1 all-gather.3
  53.7 39.2 all-gather.5
  125.3 43.1 reduce-scatter.1
where the time goes:
time: 176 us; the launch traced here: 175 us
  waiting for transfers between devices  70.9 us (40%)
  matrix products  45.8 us (26%)
  blocking collectives  22.6 us (13%)
  other arithmetic  16.2 us (9%)
  between operations  13.2 us (8%)
  local copies, waits for them, and re-layouts  6.32 us (4%)
    reduce_scatter x1, waiting for transfers between devices, body(): lax.psum_scatter(lax.dot_general(out_weight, attended, (((0,), (1,)), (()...  43.3 us
    all_gather x1, blocking collectives, body(): lax.all_gather(doc_ids, 'context', axis=0, tiled=True)  22.6 us
    dot_general x1, matrix products, body(): lax.dot_general(out_weight, attended, (((0,), (1,)), ((), ())), preferred...  16.6 us
    all_gather x1, waiting for transfers between devices, body(): lax.all_gather(key_local, 'context', axis=0, tiled=True)  16.1 us
    dot_general x1, matrix products, absorb(): jnp.einsum('tkgd,skd->kgts', grouped, key_heads, preferred_element_type=j...  15.2 us
    reduce_sum x1, other arithmetic, absorb(): running_sum = jnp.sum(weights, axis=-1)  14.9 us
    dot_general x1, matrix products, absorb(): jnp.einsum('kgts,skd->kgtd', weights.astype(jnp.bfloat16), value_heads, p...  14.1 us
    all_gather x1, waiting for transfers between devices, body(): lax.all_gather(value_local, 'context', axis=0, tiled=True)  11.4 us
  transfers between devices with their start and end apart: 3, of which 3 were waited for; matrix products, arithmetic and copies ran while one was open for 20% of the time, Pallas kernels for 0%

commit v1 on v0

v1 whole, which is shorter than its diff:
```python
import functools
import math

import jax
import jax.numpy as jnp
from jax import lax
from jax.experimental import pallas as pl
from jax.experimental.pallas import tpu as pltpu
from jax.sharding import PartitionSpec as P

H = 64
KVH = 8
HD = 128
DOC_MOST = 1024
NEG_BIG = -1e30
DOC_ROWS = 16
FOLD = HD ** (-0.5) * math.log2(math.e)


def attend_kernel(kv_count, per_kv, blocks, query_ref, docs_ref, *refs):
    kv_refs = refs[:blocks]
    out_ref, bias, key_t, value_x = refs[blocks:]
    rows = query_ref.shape[0]
    span = kv_refs[0].shape[0] - DOC_ROWS
    width = kv_count * HD
    query_docs = docs_ref[:, :1]
    lane = lax.broadcasted_iota(jnp.int32, (span, HD), 1)
    ones = jnp.where(lane == 0, 1.0, 0.0).astype(jnp.bfloat16)
    for n, kv in enumerate(kv_refs):
        key_docs = kv[span:span + DOC_ROWS, :span].astype(jnp.float32)[:1]
        same = query_docs == key_docs
        if n == 0:
            row = lax.broadcasted_iota(jnp.int32, (rows, span), 0)
            col = lax.broadcasted_iota(jnp.int32, (rows, span), 1)
            same = same & (col <= row)
        bias[:, n * span:(n + 1) * span] = jnp.where(same, 0.0, NEG_BIG)
        for g in range(kv_count):
            key_t[g, :, n * span:(n + 1) * span] = kv[:span, g * HD:(g + 1) * HD].T
            value_x[g, n * span:(n + 1) * span, :HD] = kv[:span, width + g * HD:width + (g + 1) * HD]
            value_x[g, n * span:(n + 1) * span, HD:] = ones

    for g in range(kv_count):
        def one_head(i, carry, g=g):
            at = pl.ds(pl.multiple_of((g * per_kv + i) * HD, HD), HD)
            scores = jnp.dot(query_ref[:, at], key_t[g], preferred_element_type=jnp.float32)
            scores = scores + bias[...]
            top = jnp.max(scores, axis=-1, keepdims=True)
            weights = jnp.exp2(scores * FOLD - top * FOLD).astype(jnp.bfloat16)
            both = jnp.dot(weights, value_x[g], preferred_element_type=jnp.float32)
            out_ref[:, at] = (both[:, :HD] / both[:, HD:HD + 1]).astype(jnp.bfloat16)
            return carry

        lax.fori_loop(0, per_kv, one_head, 0, unroll=2 if per_kv % 2 == 0 else 1)


def attend(query, docs, kvs, kv_count):
    rows = query.shape[0]
    per_kv = query.shape[1] // HD // kv_count
    blocks = len(kvs)
    span = kvs[0].shape[0] - DOC_ROWS
    keys = blocks * span
    heads = kv_count * per_kv
    whole = pl.BlockSpec(memory_space=pltpu.VMEM)
    return pl.pallas_call(
        functools.partial(attend_kernel, kv_count, per_kv, blocks),
        out_shape=jax.ShapeDtypeStruct(query.shape, jnp.bfloat16),
        in_specs=[whole] * (2 + blocks),
        out_specs=whole,
        scratch_shapes=[
            pltpu.VMEM((rows, keys), jnp.float32),
            pltpu.VMEM((kv_count, HD, keys), jnp.bfloat16),
            pltpu.VMEM((kv_count, keys, 2 * HD), jnp.bfloat16),
        ],
        compiler_params=pltpu.CompilerParams(vmem_limit_bytes=40 * 2**20),
        cost_estimate=pl.CostEstimate(
            flops=6 * heads * rows * keys * HD,
            bytes_accessed=4 * query.size + blocks * 2 * kvs[0].size,
            transcendentals=heads * rows * keys,
        ),
        name="attend",
    )(query, docs, *kvs)


def project_kernel(which_ref, left_ref, weight_ref, out_ref):
    out_ref[...] = jnp.dot(
        left_ref[...], weight_ref[...], preferred_element_type=jnp.float32
    ).astype(jnp.bfloat16)


def project(which, left, weight, width):
    rows, depth = left.shape
    tile = min(512, width)
    steps = width // tile
    return pl.pallas_call(
        project_kernel,
        out_shape=jax.ShapeDtypeStruct((rows, width), jnp.bfloat16),
        grid_spec=pltpu.PrefetchScalarGridSpec(
            num_scalar_prefetch=1,
            grid=(steps,),
            in_specs=[
                pl.BlockSpec((rows, depth), lambda j, w: (0, 0)),
                pl.BlockSpec((depth, tile), lambda j, w: (0, w[0] * steps + j)),
            ],
            out_specs=pl.BlockSpec((rows, tile), lambda j, w: (0, j)),
        ),
        compiler_params=pltpu.CompilerParams(vmem_limit_bytes=20 * 2**20),
        cost_estimate=pl.CostEstimate(
            flops=2 * rows * depth * width,
            bytes_accessed=2 * (depth * width + rows * width + rows * depth),
            transcendentals=0,
        ),
        name="project",
    )(which, left, weight)


def body(n_tensor, n_context, query_rows, key_rows, value_rows, doc_ids, out_weight):
    tokens_here = query_rows.shape[0]
    local_heads = query_rows.shape[1] // HD
    group_size = H // KVH
    kv_count = max(1, local_heads // group_size)
    tensor = lax.axis_index("tensor")
    first_kv = tensor * local_heads // group_size
    key_local = lax.dynamic_slice_in_dim(key_rows, first_kv * HD, kv_count * HD, 1)
    value_local = lax.dynamic_slice_in_dim(value_rows, first_kv * HD, kv_count * HD, 1)
    width = 2 * kv_count * HD
    docs = (doc_ids + 1).astype(jnp.float32)
    doc_rows = jnp.broadcast_to(
        jnp.pad(docs, (0, width - tokens_here)).astype(jnp.bfloat16)[None, :], (DOC_ROWS, width)
    )
    own = jnp.concatenate([jnp.concatenate([key_local, value_local], 1), doc_rows], 0)

    back = -(-(DOC_MOST - 1) // tokens_here)
    def up(x, by, only=None):
        pairs = [(i, i + by) for i in range(n_context) if 0 <= i + by < n_context]
        return lax.ppermute(x, "context", pairs)

    if back == 4 and n_context % 2 == 0:
        odd = lax.axis_index("context") % 2 == 1
        two = up(own, 2)
        below = lax.ppermute(own, "context", [(i, i + 1) for i in range(0, n_context, 2)])
        four = up(two, 2)
        beside = lax.ppermute(two, "context", [(i, i ^ 1) for i in range(n_context)])
        above = lax.ppermute(four, "context", [(i + 1, i) for i in range(0, n_context, 2)])
        kvs = [own, two, beside, four, jnp.where(odd, below, above)]
    else:
        kvs = [own] + [up(own, by) for by in range(1, min(back, n_context - 1) + 1)]

    query_docs = jnp.broadcast_to(docs[:, None], (tokens_here, HD))
    attended = attend(query_rows, query_docs, kvs, kv_count)

    columns = out_weight.shape[1] // n_tensor

    def reduced(rel, bit):
        if bit == 0:
            which = (tensor ^ rel).astype(jnp.int32).reshape(1)
            return project(which, attended, out_weight, columns)
        step = 1 << (bit - 1)
        sent = reduced(rel ^ step, bit - 1)
        got = lax.ppermute(sent, "tensor", [(i, i ^ step) for i in range(n_tensor)])
        mine = reduced(rel, bit - 1)
        return (mine.astype(jnp.float32) + got.astype(jnp.float32)).astype(jnp.bfloat16)

    return reduced(0, n_tensor.bit_length() - 1)


def solution(mesh):
    placed = (
        P("context", "tensor"),
        P("context", None),
        P("context", None),
        P("context"),
        P("tensor", None),
    )
    return jax.shard_map(
        functools.partial(body, mesh.shape["tensor"], mesh.shape["context"]),
        mesh=mesh,
        in_specs=placed,
        out_specs=P("context", "tensor"),
        check_vma=False,
    )
```

time: 176 us -> 94.4 us (0.54)
  matrix products: 45.8 us -> 0 us
  Pallas kernels: 0 us -> 35.1 us
  waiting for transfers between devices: 70.9 us -> 36 us
  blocking collectives: 22.6 us -> 0 us
  starting transfers between devices: 0.09 us -> 19 us
  other arithmetic: 16.2 us -> 2.71 us
  between operations: 13.2 us -> 0.15 us
  local copies, waits for them, and re-layouts: 6.32 us -> 1.09 us
    dot_general x3 -> x0, matrix products: 45.8 us -> none  [the longest x1 16.6 us: body(): lax.dot_general(out_weight, attended, (((0,), (1,)), ((), ())), preferred...]
    reduce_scatter x1 -> x0, waiting for transfers between devices: 43.3 us -> none  [body(): lax.psum_scatter(lax.dot_general(out_weight, attended, (((0,), (1,)), (()...]
    ppermute x0 -> x8, waiting for transfers between devices: none -> 36 us  [the longest x3 18 us: reduced(): got = lax.ppermute(sent, 'tensor', [(i, i ^ step) for i in range(n_tensor)])]
    pallas_call x0 -> x5, Pallas kernels: none -> 35.1 us  [the longest x4 22.1 us: project(): pl.pallas_call(project_kernel, out_shape=jax.ShapeDtypeStruct((rows, widt...]
    all_gather x2 -> x0, waiting for transfers between devices: 27.5 us -> none  [the longest x1 16.1 us: body(): lax.all_gather(key_local, 'context', axis=0, tiled=True)]
    all_gather x1 -> x0, blocking collectives: 22.6 us -> none  [body(): lax.all_gather(doc_ids, 'context', axis=0, tiled=True)]
    ppermute x0 -> x8, starting transfers between devices: none -> 19 us  [the longest x2 9.36 us: up(): return lax.ppermute(x, 'context', pairs)]
    reduce_sum x1 -> x0, other arithmetic: 14.9 us -> none  [absorb(): running_sum = jnp.sum(weights, axis=-1)]
  transfers between devices with their start and end apart: 3 -> 8, of which waited for: 3 -> 6; matrix products, arithmetic and copies ran while one was open for 20% -> 0% of each run, Pallas kernels for 0% -> 18%
where the time goes in v1:
time: 94.4 us; the launch traced here: 94 us
  waiting for transfers between devices  36 us (38%)
  Pallas kernels  35.1 us (37%)
  starting transfers between devices  19 us (20%)
  other arithmetic  2.71 us (3%)
  local copies, waits for them, and re-layouts  1.09 us (1%)
    pallas_call x4, Pallas kernels, project(): pl.pallas_call(project_kernel, out_shape=jax.ShapeDtypeStruct((rows, widt...  22.1 us
    ppermute x3, waiting for transfers between devices, reduced(): got = lax.ppermute(sent, 'tensor', [(i, i ^ step) for i in range(n_tensor)])  18 us
    pallas_call x1, Pallas kernels, attend(): pl.pallas_call(functools.partial(attend_kernel, kv_count, per_kv, blocks)...  13 us
    ppermute x2, starting transfers between devices, up(): return lax.ppermute(x, 'context', pairs)  9.36 us
    ppermute x2, waiting for transfers between devices, up(): return lax.ppermute(x, 'context', pairs)  7.49 us
    ppermute x1, waiting for transfers between devices, body(): lax.ppermute(four, 'context', [(i + 1, i) for i in range(0, n_context, 2)])  7.1 us
    ppermute x1, starting transfers between devices, body(): lax.ppermute(own, 'context', [(i, i + 1) for i in range(0, n_context, 2)])  3.41 us
    ppermute x1, waiting for transfers between devices, body(): lax.ppermute(two, 'context', [(i, i ^ 1) for i in range(n_context)])  3.09 us
  transfers between devices with their start and end apart: 8, of which 6 were waited for; matrix products, arithmetic and copies ran while one was open for 0% of the time, Pallas kernels for 18%

profile of v1, /device:TPU:0, one launch (start us, length us, event | category | flops | bytes accessed | tf_op | source)
XLA Modules:
  0.0 94.0 jit_solution(7991822796096409060)
XLA Ops:
  0.0 0.0 copy-start
  0.0 0.8 fusion
  0.8 1.0 %constant_dynamic-slice_fusion = (bf16[256,256]{1,0:T(8,128)(2,1)S(1)}, bf16[256,256]{1,0:T(8,128)(2,1)S(1)}) fusion(bf16[256,1024]{1,0:T(8,128)(2,1)} %param.7, s32[]{:T(128)S(6)} %select_n.24, bf16[256,1024]{1,0:T(8,128)(2,1)} %param.6), kind=kLoop, calls=%fused_computation.6 | loop fusion | bytes 524292 | tf_op jit(solution)/shard_map/dynamic_slice | solution.py:124
  1.8 5.0 %collective-permute-start = (bf16[272,512]{1,0:T(8,128)(2,1)S(1)}, bf16[272,512]{1,0:T(8,128)(2,1)S(1)}, u32[]{:S(2)}, u32[]{:S(2)}) collective-permute-start(bf16[272,512]{1,0:T(8,128)(2,1)S(1)} %pad_maximum_fusion.refs_0_), channel_id=1, source_target_pairs={{0,2},{1,3},{2,4},{3,5},{4,6},{5,7},{8,10},{9,11},{10,12},{11,13},... | collective-permute-start | bytes 835592 | tf_op jit(solution)/shard_map/ppermute | solution.py:135
  6.8 5.9 %collective-permute-done.refs_1_ = bf16[272,512]{1,0:T(8,128)(2,1)S(1)} collective-permute-done((bf16[272,512]{1,0:T(8,128)(2,1)S(1)}, bf16[272,512]{1,0:T(8,128)(2,1)S(1)}, u32[]{:S(2)}, u32[]{:S(2)}) %collective-permute-start) | collective-permute-done | bytes 278560 | tf_op jit(solution)/shard_map/ppermute | solution.py:135
  12.7 4.4 %collective-permute-start.2 = (bf16[272,512]{1,0:T(8,128)(2,1)S(1)}, bf16[272,512]{1,0:T(8,128)(2,1)S(1)}, u32[]{:S(2)}, u32[]{:S(2)}) collective-permute-start(bf16[272,512]{1,0:T(8,128)(2,1)S(1)} %collective-permute-done.refs_1_), channel_id=1, source_target_pairs={{0,2},{1,3},{2,4},{3,5},{4,6},{5,7},{8,10},{9,11},{10,12},{11,13},... | collective-permute-start | bytes 835592 | tf_op jit(solution)/shard_map/ppermute | solution.py:135
  17.1 3.4 %collective-permute-start.3 = (bf16[272,512]{1,0:T(8,128)(2,1)S(1)}, bf16[272,512]{1,0:T(8,128)(2,1)S(1)}, u32[]{:S(2)}, u32[]{:S(2)}) collective-permute-start(bf16[272,512]{1,0:T(8,128)(2,1)S(1)} %pad_maximum_fusion.refs_0_), channel_id=1, source_target_pairs={{0,1},{2,3},{4,5},{6,7},{8,9},{10,11},{12,13},{14,15},{16,17},{18,... | collective-permute-start | bytes 835592 | tf_op jit(solution)/shard_map/ppermute | solution.py:140
  20.5 1.6 %collective-permute-done.2.refs_3_ = bf16[272,512]{1,0:T(8,128)(2,1)S(1)} collective-permute-done((bf16[272,512]{1,0:T(8,128)(2,1)S(1)}, bf16[272,512]{1,0:T(8,128)(2,1)S(1)}, u32[]{:S(2)}, u32[]{:S(2)}) %collective-permute-start.2) | collective-permute-done | bytes 278560 | tf_op jit(solution)/shard_map/ppermute | solution.py:135
  22.1 1.3 %collective-permute-start.4 = (bf16[272,512]{1,0:T(8,128)(2,1)S(1)}, bf16[272,512]{1,0:T(8,128)(2,1)S(1)}, u32[]{:S(2)}, u32[]{:S(2)}) collective-permute-start(bf16[272,512]{1,0:T(8,128)(2,1)S(1)} %collective-permute-done.2.refs_3_), channel_id=1, source_target_pairs={{1,0},{3,2},{5,4},{7,6},{9,8},{11,10},{13,12},{15,14},{17,16},{19,... | collective-permute-start | bytes 835592 | tf_op jit(solution)/shard_map/ppermute | solution.py:143
  23.4 2.7 %collective-permute-start.1 = (bf16[272,512]{1,0:T(8,128)(2,1)S(1)}, bf16[272,512]{1,0:T(8,128)(2,1)S(1)}, u32[]{:S(2)}, u32[]{:S(2)}) collective-permute-start(bf16[272,512]{1,0:T(8,128)(2,1)S(1)} %collective-permute-done.refs_1_), channel_id=1, source_target_pairs={{0,1},{1,0},{2,3},{3,2},{4,5},{5,4},{6,7},{7,6},{8,9},{9,8},{10,11... | collective-permute-start | bytes 835592 | tf_op jit(solution)/shard_map/ppermute | solution.py:142
  26.1 0.3 collective-permute-done.3
  26.4 7.1 %collective-permute-done.4 = bf16[272,512]{1,0:T(8,128)(2,1)S(1)} collective-permute-done((bf16[272,512]{1,0:T(8,128)(2,1)S(1)}, bf16[272,512]{1,0:T(8,128)(2,1)S(1)}, u32[]{:S(2)}, u32[]{:S(2)}) %collective-permute-start.4) | collective-permute-done | bytes 278560 | tf_op jit(solution)/shard_map/ppermute | solution.py:143
  33.5 3.1 %collective-permute-done.1.refs_2_ = bf16[272,512]{1,0:T(8,128)(2,1)S(1)} collective-permute-done((bf16[272,512]{1,0:T(8,128)(2,1)S(1)}, bf16[272,512]{1,0:T(8,128)(2,1)S(1)}, u32[]{:S(2)}, u32[]{:S(2)}) %collective-permute-start.1) | collective-permute-done | bytes 278560 | tf_op jit(solution)/shard_map/ppermute | solution.py:142
  36.6 0.1 broadcast_in_dim.4.docs_ref
  36.7 0.0 copy-done
  36.7 13.0 %attend.1.left_ref = bf16[256,2048]{1,0:T(8,128)(2,1)S(1)} custom-call(bf16[256,2048]{1,0:T(8,128)(2,1)S(1)} %copy-done, f32[256,128]{1,0:T(8,128)S(1)} %broadcast_in_dim.4.docs_ref, bf16[272,512]{1,0:T(8,128)(2,1)S(1)} %pad_maximum_fusion.refs_0_, bf16[272,512]{1,0:T(8,128)(2,1)S(1)} %collective-permute-done.refs_1_, ...), custom_call_target="tpu_custom_call" | custom-call | flops 4026531840 | bytes 3489792 | tf_op jit(solution)/shard_map/attend/pallas_call | solution.py:64
  49.7 5.5 %project.7 = bf16[256,2048]{1,0:T(8,128)(2,1)S(1)} custom-call(s32[1]{0:T(128)} %bitcast.3.which_ref, bf16[256,2048]{1,0:T(8,128)(2,1)S(1)} %attend.1.left_ref, bf16[2048,8192]{1,0:T(8,128)(2,1)} %weight_ref.7), custom_call_target="tpu_custom_call" | custom-call | flops 2147483648 | bytes 10485760 | tf_op jit(solution)/shard_map/project/pallas_call | solution.py:94
  55.3 0.1 collective-permute-start.6
  55.4 5.5 %project.5 = bf16[256,2048]{1,0:T(8,128)(2,1)S(1)} custom-call(s32[1]{0:T(128)} %bitcast.1.which_ref, bf16[256,2048]{1,0:T(8,128)(2,1)S(1)} %attend.1.left_ref, bf16[2048,8192]{1,0:T(8,128)(2,1)} %weight_ref.7), custom_call_target="tpu_custom_call" | custom-call | flops 2147483648 | bytes 10485760 | tf_op jit(solution)/shard_map/project/pallas_call | solution.py:94
  60.9 0.5 collective-permute-start.5
  61.5 5.5 %project.6 = bf16[256,2048]{1,0:T(8,128)(2,1)S(1)} custom-call(s32[1]{0:T(128)} %bitcast.2.which_ref, bf16[256,2048]{1,0:T(8,128)(2,1)S(1)} %attend.1.left_ref, bf16[2048,8192]{1,0:T(8,128)(2,1)} %weight_ref.7), custom_call_target="tpu_custom_call" | custom-call | flops 2147483648 | bytes 10485760 | tf_op jit(solution)/shard_map/project/pallas_call | solution.py:94
  67.0 0.0 collective-permute-done.6
  67.0 0.4 add_convert_fusion.1
  67.4 1.6 %collective-permute-start.7 = (bf16[256,2048]{1,0:T(8,128)(2,1)S(1)}, bf16[256,2048]{1,0:T(8,128)(2,1)S(1)}, u32[]{:S(2)}, u32[]{:S(2)}) collective-permute-start(bf16[256,2048]{1,0:T(8,128)(2,1)S(1)} %add_convert_fusion.1), channel_id=1, source_target_pairs={{0,16},{8,24},{16,0},{24,8},{1,17},{9,25},{17,1},{25,9},{2,18},{10... | collective-permute-start | bytes 3145736 | tf_op jit(solution)/shard_map/ppermute | solution.py:159
  69.0 5.5 %project.4 = bf16[256,2048]{1,0:T(8,128)(2,1)S(1)} custom-call(s32[1]{0:T(128)} %bitcast.which_ref, bf16[256,2048]{1,0:T(8,128)(2,1)S(1)} %attend.1.left_ref, bf16[2048,8192]{1,0:T(8,128)(2,1)} %weight_ref.7), custom_call_target="tpu_custom_call" | custom-call | flops 2147483648 | bytes 10485760 | tf_op jit(solution)/shard_map/project/pallas_call | solution.py:94
  74.5 0.0 collective-permute-done.5
  74.5 18.0 %collective-permute-done.7 = bf16[256,2048]{1,0:T(8,128)(2,1)S(1)} collective-permute-done((bf16[256,2048]{1,0:T(8,128)(2,1)S(1)}, bf16[256,2048]{1,0:T(8,128)(2,1)S(1)}, u32[]{:S(2)}, u32[]{:S(2)}) %collective-permute-start.7) | collective-permute-done | bytes 1048608 | tf_op jit(solution)/shard_map/ppermute | solution.py:159
  92.5 1.5 %add_convert_fusion = bf16[256,2048]{1,0:T(8,128)(2,1)} fusion(bf16[256,2048]{1,0:T(8,128)(2,1)S(1)} %collective-permute-done.7, bf16[256,2048]{1,0:T(8,128)(2,1)S(1)} %collective-permute-done.5, bf16[256,2048]{1,0:T(8,128)(2,1)S(1)} %project.4), kind=kLoop, calls=%fused_computation | loop fusion | flops 4194304 | bytes 4194304 | tf_op jit(solution)/shard_map/convert_element_type | solution.py:161
  (4 shorter events, 0.1 us)
Async XLA Ops:
  0.0 36.7 %copy-start = (bf16[256,2048]{1,0:T(8,128)(2,1)S(1)}, bf16[256,2048]{1,0:T(8,128)(2,1)}, u32[]{:S(2)}) copy-start(bf16[256,2048]{1,0:T(8,128)(2,1)} %query_ref.1) | copy-start | bytes 3145732
  1.8 10.9 %collective-permute-start = (bf16[272,512]{1,0:T(8,128)(2,1)S(1)}, bf16[272,512]{1,0:T(8,128)(2,1)S(1)}, u32[]{:S(2)}, u32[]{:S(2)}) collective-permute-start(bf16[272,512]{1,0:T(8,128)(2,1)S(1)} %pad_maximum_fusion.refs_0_), channel_id=1, source_target_pairs={{0,2},{1,3},{2,4},{3,5},{4,6},{5,7},{8,10},{9,11},{10,12},{11,13},... | collective-permute-start | bytes 835592 | tf_op jit(solution)/shard_map/ppermute | solution.py:135
  12.7 9.4 %collective-permute-start.2 = (bf16[272,512]{1,0:T(8,128)(2,1)S(1)}, bf16[272,512]{1,0:T(8,128)(2,1)S(1)}, u32[]{:S(2)}, u32[]{:S(2)}) collective-permute-start(bf16[272,512]{1,0:T(8,128)(2,1)S(1)} %collective-permute-done.refs_1_), channel_id=1, source_target_pairs={{0,2},{1,3},{2,4},{3,5},{4,6},{5,7},{8,10},{9,11},{10,12},{11,13},... | collective-permute-start | bytes 835592 | tf_op jit(solution)/shard_map/ppermute | solution.py:135
  17.1 9.3 %collective-permute-start.3 = (bf16[272,512]{1,0:T(8,128)(2,1)S(1)}, bf16[272,512]{1,0:T(8,128)(2,1)S(1)}, u32[]{:S(2)}, u32[]{:S(2)}) collective-permute-start(bf16[272,512]{1,0:T(8,128)(2,1)S(1)} %pad_maximum_fusion.refs_0_), channel_id=1, source_target_pairs={{0,1},{2,3},{4,5},{6,7},{8,9},{10,11},{12,13},{14,15},{16,17},{18,... | collective-permute-start | bytes 835592 | tf_op jit(solution)/shard_map/ppermute | solution.py:140
  22.1 11.4 %collective-permute-start.4 = (bf16[272,512]{1,0:T(8,128)(2,1)S(1)}, bf16[272,512]{1,0:T(8,128)(2,1)S(1)}, u32[]{:S(2)}, u32[]{:S(2)}) collective-permute-start(bf16[272,512]{1,0:T(8,128)(2,1)S(1)} %collective-permute-done.2.refs_3_), channel_id=1, source_target_pairs={{1,0},{3,2},{5,4},{7,6},{9,8},{11,10},{13,12},{15,14},{17,16},{19,... | collective-permute-start | bytes 835592 | tf_op jit(solution)/shard_map/ppermute | solution.py:143
  23.4 13.2 %collective-permute-start.1 = (bf16[272,512]{1,0:T(8,128)(2,1)S(1)}, bf16[272,512]{1,0:T(8,128)(2,1)S(1)}, u32[]{:S(2)}, u32[]{:S(2)}) collective-permute-start(bf16[272,512]{1,0:T(8,128)(2,1)S(1)} %collective-permute-done.refs_1_), channel_id=1, source_target_pairs={{0,1},{1,0},{2,3},{3,2},{4,5},{5,4},{6,7},{7,6},{8,9},{9,8},{10,11... | collective-permute-start | bytes 835592 | tf_op jit(solution)/shard_map/ppermute | solution.py:142
  55.3 11.7 %collective-permute-start.6 = (bf16[256,2048]{1,0:T(8,128)(2,1)S(1)}, bf16[256,2048]{1,0:T(8,128)(2,1)S(1)}, u32[]{:S(2)}, u32[]{:S(2)}) collective-permute-start(bf16[256,2048]{1,0:T(8,128)(2,1)S(1)} %project.7), channel_id=1, source_target_pairs={{0,8},{8,0},{16,24},{24,16},{1,9},{9,1},{17,25},{25,17},{2,10},{10... | collective-permute-start | bytes 3145736 | tf_op jit(solution)/shard_map/ppermute | solution.py:159
  60.9 13.6 %collective-permute-start.5 = (bf16[256,2048]{1,0:T(8,128)(2,1)S(1)}, bf16[256,2048]{1,0:T(8,128)(2,1)S(1)}, u32[]{:S(2)}, u32[]{:S(2)}) collective-permute-start(bf16[256,2048]{1,0:T(8,128)(2,1)S(1)} %project.5), channel_id=1, source_target_pairs={{0,8},{8,0},{16,24},{24,16},{1,9},{9,1},{17,25},{25,17},{2,10},{10... | collective-permute-start | bytes 3145736 | tf_op jit(solution)/shard_map/ppermute | solution.py:159
  67.4 25.2 %collective-permute-start.7 = (bf16[256,2048]{1,0:T(8,128)(2,1)S(1)}, bf16[256,2048]{1,0:T(8,128)(2,1)S(1)}, u32[]{:S(2)}, u32[]{:S(2)}) collective-permute-start(bf16[256,2048]{1,0:T(8,128)(2,1)S(1)} %add_convert_fusion.1), channel_id=1, source_target_pairs={{0,16},{8,24},{16,0},{24,8},{1,17},{9,25},{17,1},{25,9},{2,18},{10... | collective-permute-start | bytes 3145736 | tf_op jit(solution)/shard_map/ppermute | solution.py:159

commit v2 on v1

--- a/solution.py
+++ b/solution.py
@@ -17,19 +17,33 @@
 FOLD = HD ** (-0.5) * math.log2(math.e)
 
 
-def attend_kernel(kv_count, per_kv, blocks, query_ref, docs_ref, *refs):
-    kv_refs = refs[:blocks]
-    out_ref, bias, key_t, value_x = refs[blocks:]
+def attend_kernel(kv_count, per_kv, blocks, causal, carried, last, query_ref, docs_ref, *refs):
+    kv_refs, refs = refs[:blocks], refs[blocks:]
+    if carried:
+        before_ref, refs = refs[0], refs[1:]
+    if last:
+        which_ref, weight_ref, refs = refs[0], refs[1], refs[2:]
+    out_ref, refs = refs[0], refs[1:]
+    if last:
+        part_ref, refs = refs[0], refs[1:]
+    bias, key_t, value_x = refs[:3]
     rows = query_ref.shape[0]
     span = kv_refs[0].shape[0] - DOC_ROWS
     width = kv_count * HD
+    if last:
+        held, sem = refs[3:]
+        columns = held.shape[1]
+        fetch = pltpu.make_async_copy(
+            weight_ref.at[:, pl.ds(pl.multiple_of(which_ref[0] * columns, columns), columns)], held, sem
+        )
+        fetch.start()
     query_docs = docs_ref[:, :1]
     lane = lax.broadcasted_iota(jnp.int32, (span, HD), 1)
     ones = jnp.where(lane == 0, 1.0, 0.0).astype(jnp.bfloat16)
     for n, kv in enumerate(kv_refs):
         key_docs = kv[span:span + DOC_ROWS, :span].astype(jnp.float32)[:1]
         same = query_docs == key_docs
-        if n == 0:
+        if causal:
             row = lax.broadcasted_iota(jnp.int32, (rows, span), 0)
             col = lax.broadcasted_iota(jnp.int32, (rows, span), 1)
             same = same & (col <= row)
@@ -39,46 +53,85 @@
             value_x[g, n * span:(n + 1) * span, :HD] = kv[:span, width + g * HD:width + (g + 1) * HD]
             value_x[g, n * span:(n + 1) * span, HD:] = ones
 
+    stat = lax.broadcasted_iota(jnp.int32, (rows, HD), 1)
     for g in range(kv_count):
         def one_head(i, carry, g=g):
-            at = pl.ds(pl.multiple_of((g * per_kv + i) * HD, HD), HD)
+            head = g * per_kv + i
+            at = pl.ds(pl.multiple_of(head * HD, HD), HD)
             scores = jnp.dot(query_ref[:, at], key_t[g], preferred_element_type=jnp.float32)
             scores = scores + bias[...]
             top = jnp.max(scores, axis=-1, keepdims=True)
+            if carried:
+                old_top = before_ref[head, :, HD + 1:HD + 2]
+                top = jnp.maximum(top, old_top)
             weights = jnp.exp2(scores * FOLD - top * FOLD).astype(jnp.bfloat16)
             both = jnp.dot(weights, value_x[g], preferred_element_type=jnp.float32)
-            out_ref[:, at] = (both[:, :HD] / both[:, HD:HD + 1]).astype(jnp.bfloat16)
+            numer, total = both[:, :HD], both[:, HD:]
+            if carried:
+                fade = jnp.exp2(old_top * FOLD - top * FOLD)
+                numer = numer + fade * before_ref[head, :, :HD]
+                total = total + fade * before_ref[head, :, HD:]
+            if last:
+                out_ref[:, at] = (numer / total[:, :1]).astype(jnp.bfloat16)
+            else:
+                out_ref[head, :, :HD] = numer
+                out_ref[head, :, HD:] = jnp.where(stat == 1, top, total)
             return carry
 
-        lax.fori_loop(0, per_kv, one_head, 0, unroll=2 if per_kv % 2 == 0 else 1)
-
-
-def attend(query, docs, kvs, kv_count):
+        lax.fori_loop(0, per_kv, one_head, 0, unroll=4 if per_kv % 4 == 0 else 1)
+    if last:
+        fetch.wait()
+        part_ref[...] = jnp.dot(
+            out_ref[...], held[...], preferred_element_type=jnp.float32
+        ).astype(jnp.bfloat16)
+
+
+def attend(query, docs, kvs, kv_count, causal=False, before=None, last=None):
     rows = query.shape[0]
-    per_kv = query.shape[1] // HD // kv_count
+    heads = query.shape[1] // HD
+    per_kv = heads // kv_count
     blocks = len(kvs)
-    span = kvs[0].shape[0] - DOC_ROWS
-    keys = blocks * span
-    heads = kv_count * per_kv
+    keys = blocks * (kvs[0].shape[0] - DOC_ROWS)
     whole = pl.BlockSpec(memory_space=pltpu.VMEM)
+    scratch = [
+        pltpu.VMEM((rows, keys), jnp.float32),
+        pltpu.VMEM((kv_count, HD, keys), jnp.bfloat16),
+        pltpu.VMEM((kv_count, keys, 2 * HD), jnp.bfloat16),
+    ]
+    args, specs = [query, docs, *kvs], [whole] * (2 + blocks)
+    if before is not None:
+        args, specs = args + [before], specs + [whole]
+    flops = 6 * heads * rows * keys * HD
+    if last is None:
+        outs = jax.ShapeDtypeStruct((heads, rows, 2 * HD), jnp.float32)
+        out_specs = whole
+    else:
+        which, weight, columns = last
+        args = args + [which, weight]
+        specs = specs + [pl.BlockSpec(memory_space=pltpu.SMEM), pl.BlockSpec(memory_space=pl.ANY)]
+        outs = (
+            jax.ShapeDtypeStruct(query.shape, jnp.bfloat16),
+            jax.ShapeDtypeStruct((rows, columns), jnp.bfloat16),
+        )
+        out_specs = (whole, whole)
+        scratch += [pltpu.VMEM((weight.shape[0], columns), jnp.bfloat16), pltpu.SemaphoreType.DMA]
+        flops += 2 * rows * query.shape[1] * columns
     return pl.pallas_call(
-        functools.partial(attend_kernel, kv_count, per_kv, blocks),
-        out_shape=jax.ShapeDtypeStruct(query.shape, jnp.bfloat16),
-        in_specs=[whole] * (2 + blocks),
-        out_specs=whole,
-        scratch_shapes=[
-            pltpu.VMEM((rows, keys), jnp.float32),
-            pltpu.VMEM((kv_count, HD, keys), jnp.bfloat16),
-            pltpu.VMEM((kv_count, keys, 2 * HD), jnp.bfloat16),
-        ],
-        compiler_params=pltpu.CompilerParams(vmem_limit_bytes=40 * 2**20),
+        functools.partial(
+            attend_kernel, kv_count, per_kv, blocks, causal, before is not None, last is not None
+        ),
+        out_shape=outs,
+        in_specs=specs,
+        out_specs=out_specs,
+        scratch_shapes=scratch,
+        compiler_params=pltpu.CompilerParams(vmem_limit_bytes=44 * 2**20),
         cost_estimate=pl.CostEstimate(
-            flops=6 * heads * rows * keys * HD,
+            flops=flops,
             bytes_accessed=4 * query.size + blocks * 2 * kvs[0].size,
             transcendentals=heads * rows * keys,
         ),
         name="attend",
-    )(query, docs, *kvs)
+    )(*args)
 
 
 def project_kernel(which_ref, left_ref, weight_ref, out_ref):
@@ -89,7 +142,7 @@
 
 def project(which, left, weight, width):
     rows, depth = left.shape
-    tile = min(512, width)
+    tile = min(1024, width)
     steps = width // tile
     return pl.pallas_call(
         project_kernel,
@@ -103,7 +156,7 @@
             ],
             out_specs=pl.BlockSpec((rows, tile), lambda j, w: (0, j)),
         ),
-        compiler_params=pltpu.CompilerParams(vmem_limit_bytes=20 * 2**20),
+        compiler_params=pltpu.CompilerParams(vmem_limit_bytes=24 * 2**20),
         cost_estimate=pl.CostEstimate(
             flops=2 * rows * depth * width,
             bytes_accessed=2 * (depth * width + rows * width + rows * depth),
@@ -134,28 +187,42 @@
         pairs = [(i, i + by) for i in range(n_context) if 0 <= i + by < n_context]
         return lax.ppermute(x, "context", pairs)
 
+    columns = out_weight.shape[1] // n_tensor
+
+    def chosen(rel):
+        return (tensor ^ rel).astype(jnp.int32).reshape(1)
+
+    query_docs = jnp.broadcast_to(docs[:, None], (tokens_here, HD))
+    far = n_tensor - 1
+    last = (chosen(far), out_weight, columns)
     if back == 4 and n_context % 2 == 0:
         odd = lax.axis_index("context") % 2 == 1
         two = up(own, 2)
         below = lax.ppermute(own, "context", [(i, i + 1) for i in range(0, n_context, 2)])
+        state = attend(query_rows, query_docs, [own], kv_count, causal=True)
+        two, below, state = lax.optimization_barrier((two, below, state))
         four = up(two, 2)
         beside = lax.ppermute(two, "context", [(i, i ^ 1) for i in range(n_context)])
+        state = attend(query_rows, query_docs, [two], kv_count, before=state)
+        four, beside, state = lax.optimization_barrier((four, beside, state))
         above = lax.ppermute(four, "context", [(i + 1, i) for i in range(0, n_context, 2)])
-        kvs = [own, two, beside, four, jnp.where(odd, below, above)]
+        kvs = [beside, four, jnp.where(odd, below, above)]
     else:
-        kvs = [own] + [up(own, by) for by in range(1, min(back, n_context - 1) + 1)]
-
-    query_docs = jnp.broadcast_to(docs[:, None], (tokens_here, HD))
-    attended = attend(query_rows, query_docs, kvs, kv_count)
-
-    columns = out_weight.shape[1] // n_tensor
+        state = attend(query_rows, query_docs, [own], kv_count, causal=True)
+        kvs = [up(own, by) for by in range(1, min(back, n_context - 1) + 1)]
+    attended, first_part = attend(
+        query_rows, query_docs, kvs, kv_count, before=state, last=last
+    )
 
     def reduced(rel, bit):
+        nonlocal attended
         if bit == 0:
-            which = (tensor ^ rel).astype(jnp.int32).reshape(1)
-            return project(which, attended, out_weight, columns)
+            if rel == far:
+                return first_part
+            return project(chosen(rel), attended, out_weight, columns)
         step = 1 << (bit - 1)
         sent = reduced(rel ^ step, bit - 1)
+        attended, sent = lax.optimization_barrier((attended, sent))
         got = lax.ppermute(sent, "tensor", [(i, i ^ step) for i in range(n_tensor)])
         mine = reduced(rel, bit - 1)
         return (mine.astype(jnp.float32) + got.astype(jnp.float32)).astype(jnp.bfloat16)

time: 94.4 us -> 90 us (0.953)
  waiting for transfers between devices: 36 us -> 27.6 us
  local copies, waits for them, and re-layouts: 1.09 us -> 6.44 us
  starting transfers between devices: 19 us -> 18 us
    pallas_call x4 -> x3, Pallas kernels: 22.1 us -> 14.3 us  [project(): pl.pallas_call(project_kernel, out_shape=jax.ShapeDtypeStruct((rows, widt...]
    ppermute x2, waiting for transfers between devices: 7.49 us -> 0.01 us  [up(): return lax.ppermute(x, 'context', pairs)]
    pallas_call x1 -> x3, Pallas kernels: 13 us -> 20.5 us  [attend(): pl.pallas_call(functools.partial(attend_kernel, kv_count, per_kv, blocks,...]
    unnamed x2 -> x8, local copies, waits for them, and re-layouts: 0.01 us -> 5.35 us
    ppermute x1, waiting for transfers between devices: 3.09 us -> 0.01 us  [body(): lax.ppermute(two, 'context', [(i, i ^ 1) for i in range(n_context)])]
    ppermute x1, waiting for transfers between devices: 0.31 us -> 1.66 us  [body(): lax.ppermute(own, 'context', [(i, i + 1) for i in range(0, n_context, 2)])]
  transfers between devices with their start and end apart: 8 -> 8, of which waited for: 6 -> 3; matrix products, arithmetic and copies ran while one was open for 0% -> 0% of each run, Pallas kernels for 18% -> 21%
where the time goes in v2:
time: 90 us; the launch traced here: 89.7 us
  Pallas kernels  34.8 us (39%)
  waiting for transfers between devices  27.6 us (31%)
  starting transfers between devices  18 us (20%)
  local copies, waits for them, and re-layouts  6.44 us (7%)
  other arithmetic  2.64 us (3%)
    pallas_call x3, Pallas kernels, attend(): pl.pallas_call(functools.partial(attend_kernel, kv_count, per_kv, blocks,...  20.5 us
    ppermute x3, waiting for transfers between devices, reduced(): got = lax.ppermute(sent, 'tensor', [(i, i ^ step) for i in range(n_tensor)])  18.8 us
    pallas_call x3, Pallas kernels, project(): pl.pallas_call(project_kernel, out_shape=jax.ShapeDtypeStruct((rows, widt...  14.3 us
    ppermute x2, starting transfers between devices, up(): return lax.ppermute(x, 'context', pairs)  8.45 us
    ppermute x1, waiting for transfers between devices, body(): lax.ppermute(four, 'context', [(i + 1, i) for i in range(0, n_context, 2)])  7.1 us
    unnamed x8, local copies, waits for them, and re-layouts  5.35 us
    ppermute x1, starting transfers between devices, body(): lax.ppermute(own, 'context', [(i, i + 1) for i in range(0, n_context, 2)])  3.41 us
    ppermute x1, starting transfers between devices, body(): lax.ppermute(two, 'context', [(i, i ^ 1) for i in range(n_context)])  2.55 us
  transfers between devices with their start and end apart: 8, of which 3 were waited for; matrix products, arithmetic and copies ran while one was open for 0% of the time, Pallas kernels for 21%

profile of v2, /device:TPU:0, one launch (start us, length us, event | category | flops | bytes accessed | tf_op | source)
XLA Modules:
  0.0 89.7 jit_solution(8122111373181854623)
XLA Ops:
  0.0 0.7 fusion
  0.7 1.0 %constant_dynamic-slice_fusion = (bf16[256,256]{1,0:T(8,128)(2,1)S(1)}, bf16[256,256]{1,0:T(8,128)(2,1)S(1)}) fusion(bf16[256,1024]{1,0:T(8,128)(2,1)} %param.7, s32[]{:T(128)S(6)} %select_n.24, bf16[256,1024]{1,0:T(8,128)(2,1)} %param.6), kind=kLoop, calls=%fused_computation.6 | loop fusion | bytes 524292 | tf_op jit(solution)/shard_map/dynamic_slice | solution.py:177
  1.7 5.0 %collective-permute-start = (bf16[272,512]{1,0:T(8,128)(2,1)S(1)}, bf16[272,512]{1,0:T(8,128)(2,1)S(1)}, u32[]{:S(2)}, u32[]{:S(2)}) collective-permute-start(bf16[272,512]{1,0:T(8,128)(2,1)S(1)} %pad_maximum_fusion.refs_0_), channel_id=1, source_target_pairs={{0,2},{1,3},{2,4},{3,5},{4,6},{5,7},{8,10},{9,11},{10,12},{11,13},... | collective-permute-start | bytes 835592 | tf_op jit(solution)/shard_map/ppermute | solution.py:188
  6.7 3.4 %collective-permute-start.1 = (bf16[272,512]{1,0:T(8,128)(2,1)S(1)}, bf16[272,512]{1,0:T(8,128)(2,1)S(1)}, u32[]{:S(2)}, u32[]{:S(2)}) collective-permute-start(bf16[272,512]{1,0:T(8,128)(2,1)S(1)} %pad_maximum_fusion.refs_0_), channel_id=1, source_target_pairs={{0,1},{2,3},{4,5},{6,7},{8,9},{10,11},{12,13},{14,15},{16,17},{18,... | collective-permute-start | bytes 835592 | tf_op jit(solution)/shard_map/ppermute | solution.py:201
  10.1 0.1 broadcast_in_dim.4.docs_ref
  10.2 0.0 copy-start.2
  10.2 1.2 %copy-done.2 = bf16[256,2048]{1,0:T(8,128)(2,1)S(1)} copy-done((bf16[256,2048]{1,0:T(8,128)(2,1)S(1)}, bf16[256,2048]{1,0:T(8,128)(2,1)}, u32[]{:S(2)}) %copy-start.2) | copy-done | bytes 1048600
  11.5 2.6 %attend.3.refs_1_ = f32[16,256,256]{2,1,0:T(8,128)S(1)} custom-call(bf16[256,2048]{1,0:T(8,128)(2,1)S(1)} %copy-done.2, f32[256,128]{1,0:T(8,128)S(1)} %broadcast_in_dim.4.docs_ref, bf16[272,512]{1,0:T(8,128)(2,1)S(1)} %pad_maximum_fusion.refs_0_), custom_call_target="tpu_custom_call" | custom-call | flops 805306368 | bytes 2375680 | tf_op jit(solution)/shard_map/attend/pallas_call | solution.py:119
  14.0 0.0 copy-start.3
  14.1 0.0 collective-permute-done.refs_0_
  14.1 1.7 %collective-permute-done.1 = bf16[272,512]{1,0:T(8,128)(2,1)S(1)} collective-permute-done((bf16[272,512]{1,0:T(8,128)(2,1)S(1)}, bf16[272,512]{1,0:T(8,128)(2,1)S(1)}, u32[]{:S(2)}, u32[]{:S(2)}) %collective-permute-start.1) | collective-permute-done | bytes 278560 | tf_op jit(solution)/shard_map/ppermute | solution.py:201
  15.7 3.5 %collective-permute-start.2 = (bf16[272,512]{1,0:T(8,128)(2,1)S(1)}, bf16[272,512]{1,0:T(8,128)(2,1)S(1)}, u32[]{:S(2)}, u32[]{:S(2)}) collective-permute-start(bf16[272,512]{1,0:T(8,128)(2,1)S(1)} %collective-permute-done.refs_0_), channel_id=1, source_target_pairs={{0,2},{1,3},{2,4},{3,5},{4,6},{5,7},{8,10},{9,11},{10,12},{11,13},... | collective-permute-start | bytes 835592 | tf_op jit(solution)/shard_map/ppermute | solution.py:188
  19.2 2.5 %collective-permute-start.3 = (bf16[272,512]{1,0:T(8,128)(2,1)S(1)}, bf16[272,512]{1,0:T(8,128)(2,1)S(1)}, u32[]{:S(2)}, u32[]{:S(2)}) collective-permute-start(bf16[272,512]{1,0:T(8,128)(2,1)S(1)} %collective-permute-done.refs_0_), channel_id=1, source_target_pairs={{0,1},{1,0},{2,3},{3,2},{4,5},{5,4},{6,7},{7,6},{8,9},{9,8},{10,11... | collective-permute-start | bytes 835592 | tf_op jit(solution)/shard_map/ppermute | solution.py:205
  21.8 6.6 %attend.4.refs_3_ = f32[16,256,256]{2,1,0:T(8,128)S(1)} custom-call(bf16[256,2048]{1,0:T(8,128)(2,1)S(1)} %copy-done.2, f32[256,128]{1,0:T(8,128)S(1)} %broadcast_in_dim.4.docs_ref, bf16[272,512]{1,0:T(8,128)(2,1)S(1)} %collective-permute-done.refs_0_, f32[16,256,256]{2,1,0:T(8,128)S(1)} %attend.3.refs_1_), custom_call_target="tpu_custom_call" | custom-call | flops 805306368 | bytes 2375680 | tf_op jit(solution)/shard_map/attend/pallas_call | solution.py:119
  28.4 0.0 copy-start
  28.4 1.9 %copy-done = f32[16,256,256]{2,1,0:T(8,128)} copy-done((f32[16,256,256]{2,1,0:T(8,128)}, f32[16,256,256]{2,1,0:T(8,128)S(1)}, u32[]{:S(2)}) %copy-start) | copy-done | bytes 4194328
  30.3 0.0 collective-permute-done.2.refs_1_
  30.3 0.0 collective-permute-done.3.refs_0_
  30.3 1.5 %collective-permute-start.4 = (bf16[272,512]{1,0:T(8,128)(2,1)S(1)}, bf16[272,512]{1,0:T(8,128)(2,1)S(1)}, u32[]{:S(2)}, u32[]{:S(2)}) collective-permute-start(bf16[272,512]{1,0:T(8,128)(2,1)S(1)} %collective-permute-done.2.refs_1_), channel_id=1, source_target_pairs={{1,0},{3,2},{5,4},{7,6},{9,8},{11,10},{13,12},{15,14},{17,16},{19,... | collective-permute-start | bytes 835592 | tf_op jit(solution)/shard_map/ppermute | solution.py:208
  31.8 7.1 %collective-permute-done.4 = bf16[272,512]{1,0:T(8,128)(2,1)S(1)} collective-permute-done((bf16[272,512]{1,0:T(8,128)(2,1)S(1)}, bf16[272,512]{1,0:T(8,128)(2,1)S(1)}, u32[]{:S(2)}, u32[]{:S(2)}) %collective-permute-start.4) | collective-permute-done | bytes 278560 | tf_op jit(solution)/shard_map/ppermute | solution.py:208
  38.9 0.0 copy-done.3
  39.0 0.0 copy-start.1
  39.0 2.2 %copy-done.1 = f32[16,256,256]{2,1,0:T(8,128)S(1)} copy-done((f32[16,256,256]{2,1,0:T(8,128)S(1)}, f32[16,256,256]{2,1,0:T(8,128)}, u32[]{:S(2)}) %copy-start.1) | copy-done | bytes 4194328
  41.1 11.3 %attend.5 = (bf16[256,2048]{1,0:T(8,128)(2,1)S(1)}, bf16[256,2048]{1,0:T(8,128)(2,1)}) custom-call(bf16[256,2048]{1,0:T(8,128)(2,1)S(1)} %copy-done.3, f32[256,128]{1,0:T(8,128)S(1)} %broadcast_in_dim.4.docs_ref, bf16[272,512]{1,0:T(8,128)(2,1)S(1)} %collective-permute-done.3.refs_0_, bf16[272,512]{1,0:T(8,128)(2,1)S(1)} %collective-permute-done.2.refs_1_, ...), custom_call_target="tpu_custom_call" | custom-call | flops 4563402752 | bytes 2932736 | tf_op jit(solution)/shard_map/attend/pallas_call | solution.py:119
  52.4 0.1 collective-permute-start.5
  52.5 4.8 %project.3 = bf16[256,2048]{1,0:T(8,128)(2,1)S(1)} custom-call(s32[1]{0:T(128)} %bitcast.2.which_ref, bf16[256,2048]{1,0:T(8,128)(2,1)S(1)} %get-tuple-element.26.left_ref, bf16[2048,8192]{1,0:T(8,128)(2,1)} %weight_ref.5), custom_call_target="tpu_custom_call" | custom-call | flops 2147483648 | bytes 10485760 | tf_op jit(solution)/shard_map/project/pallas_call | solution.py:147
  57.3 0.0 collective-permute-done.5
  57.3 0.4 add_convert_fusion.2
  57.7 4.8 %project.4 = bf16[256,2048]{1,0:T(8,128)(2,1)S(1)} custom-call(s32[1]{0:T(128)} %bitcast.3.which_ref, bf16[256,2048]{1,0:T(8,128)(2,1)S(1)} %get-tuple-element.26.left_ref, bf16[2048,8192]{1,0:T(8,128)(2,1)} %weight_ref.5), custom_call_target="tpu_custom_call" | custom-call | flops 2147483648 | bytes 10485760 | tf_op jit(solution)/shard_map/project/pallas_call | solution.py:147
  62.5 0.5 collective-permute-start.6
  63.1 1.5 %collective-permute-start.7 = (bf16[256,2048]{1,0:T(8,128)(2,1)S(1)}, bf16[256,2048]{1,0:T(8,128)(2,1)S(1)}, u32[]{:S(2)}, u32[]{:S(2)}) collective-permute-start(bf16[256,2048]{1,0:T(8,128)(2,1)S(1)} %add_convert_fusion.2), channel_id=1, source_target_pairs={{0,16},{8,24},{16,0},{24,8},{1,17},{9,25},{17,1},{25,9},{2,18},{10... | collective-permute-start | bytes 3145736 | tf_op jit(solution)/shard_map/ppermute | solution.py:226
  64.6 4.8 %project.5 = bf16[256,2048]{1,0:T(8,128)(2,1)S(1)} custom-call(s32[1]{0:T(128)} %bitcast.which_ref, bf16[256,2048]{1,0:T(8,128)(2,1)S(1)} %get-tuple-element.26.left_ref, bf16[2048,8192]{1,0:T(8,128)(2,1)} %weight_ref.5), custom_call_target="tpu_custom_call" | custom-call | flops 2147483648 | bytes 10485760 | tf_op jit(solution)/shard_map/project/pallas_call | solution.py:147
  69.4 0.0 collective-permute-done.6
  69.4 18.8 %collective-permute-done.7 = bf16[256,2048]{1,0:T(8,128)(2,1)S(1)} collective-permute-done((bf16[256,2048]{1,0:T(8,128)(2,1)S(1)}, bf16[256,2048]{1,0:T(8,128)(2,1)S(1)}, u32[]{:S(2)}, u32[]{:S(2)}) %collective-permute-start.7) | collective-permute-done | bytes 1048608 | tf_op jit(solution)/shard_map/ppermute | solution.py:226
  88.2 1.5 %add_convert_fusion = bf16[256,2048]{1,0:T(8,128)(2,1)} fusion(bf16[256,2048]{1,0:T(8,128)(2,1)S(1)} %collective-permute-done.7, bf16[256,2048]{1,0:T(8,128)(2,1)S(1)} %collective-permute-done.6, bf16[256,2048]{1,0:T(8,128)(2,1)S(1)} %project.5), kind=kLoop, calls=%fused_computation | loop fusion | flops 4194304 | bytes 4194304 | tf_op jit(solution)/shard_map/convert_element_type | solution.py:228
  (4 shorter events, 0.1 us)
Async XLA Ops:
  1.7 12.3 %collective-permute-start = (bf16[272,512]{1,0:T(8,128)(2,1)S(1)}, bf16[272,512]{1,0:T(8,128)(2,1)S(1)}, u32[]{:S(2)}, u32[]{:S(2)}) collective-permute-start(bf16[272,512]{1,0:T(8,128)(2,1)S(1)} %pad_maximum_fusion.refs_0_), channel_id=1, source_target_pairs={{0,2},{1,3},{2,4},{3,5},{4,6},{5,7},{8,10},{9,11},{10,12},{11,13},... | collective-permute-start | bytes 835592 | tf_op jit(solution)/shard_map/ppermute | solution.py:188
  6.7 9.0 %collective-permute-start.1 = (bf16[272,512]{1,0:T(8,128)(2,1)S(1)}, bf16[272,512]{1,0:T(8,128)(2,1)S(1)}, u32[]{:S(2)}, u32[]{:S(2)}) collective-permute-start(bf16[272,512]{1,0:T(8,128)(2,1)S(1)} %pad_maximum_fusion.refs_0_), channel_id=1, source_target_pairs={{0,1},{2,3},{4,5},{6,7},{8,9},{10,11},{12,13},{14,15},{16,17},{18,... | collective-permute-start | bytes 835592 | tf_op jit(solution)/shard_map/ppermute | solution.py:201
  10.2 1.2 %copy-start.2 = (bf16[256,2048]{1,0:T(8,128)(2,1)S(1)}, bf16[256,2048]{1,0:T(8,128)(2,1)}, u32[]{:S(2)}) copy-start(bf16[256,2048]{1,0:T(8,128)(2,1)} %query_ref.5) | copy-start | bytes 3145732
  14.0 24.9 %copy-start.3 = (bf16[256,2048]{1,0:T(8,128)(2,1)S(1)}, bf16[256,2048]{1,0:T(8,128)(2,1)}, u32[]{:S(2)}) copy-start(bf16[256,2048]{1,0:T(8,128)(2,1)} %query_ref.5) | copy-start | bytes 3145732
  15.7 14.6 %collective-permute-start.2 = (bf16[272,512]{1,0:T(8,128)(2,1)S(1)}, bf16[272,512]{1,0:T(8,128)(2,1)S(1)}, u32[]{:S(2)}, u32[]{:S(2)}) collective-permute-start(bf16[272,512]{1,0:T(8,128)(2,1)S(1)} %collective-permute-done.refs_0_), channel_id=1, source_target_pairs={{0,2},{1,3},{2,4},{3,5},{4,6},{5,7},{8,10},{9,11},{10,12},{11,13},... | collective-permute-start | bytes 835592 | tf_op jit(solution)/shard_map/ppermute | solution.py:188
  19.2 11.1 %collective-permute-start.3 = (bf16[272,512]{1,0:T(8,128)(2,1)S(1)}, bf16[272,512]{1,0:T(8,128)(2,1)S(1)}, u32[]{:S(2)}, u32[]{:S(2)}) collective-permute-start(bf16[272,512]{1,0:T(8,128)(2,1)S(1)} %collective-permute-done.refs_0_), channel_id=1, source_target_pairs={{0,1},{1,0},{2,3},{3,2},{4,5},{5,4},{6,7},{7,6},{8,9},{9,8},{10,11... | collective-permute-start | bytes 835592 | tf_op jit(solution)/shard_map/ppermute | solution.py:205
  28.4 1.9 %copy-start = (f32[16,256,256]{2,1,0:T(8,128)}, f32[16,256,256]{2,1,0:T(8,128)S(1)}, u32[]{:S(2)}) copy-start(f32[16,256,256]{2,1,0:T(8,128)S(1)} %attend.4.refs_3_) | copy-start | bytes 12582916
  30.3 8.6 %collective-permute-start.4 = (bf16[272,512]{1,0:T(8,128)(2,1)S(1)}, bf16[272,512]{1,0:T(8,128)(2,1)S(1)}, u32[]{:S(2)}, u32[]{:S(2)}) collective-permute-start(bf16[272,512]{1,0:T(8,128)(2,1)S(1)} %collective-permute-done.2.refs_1_), channel_id=1, source_target_pairs={{1,0},{3,2},{5,4},{7,6},{9,8},{11,10},{13,12},{15,14},{17,16},{19,... | collective-permute-start | bytes 835592 | tf_op jit(solution)/shard_map/ppermute | solution.py:208
  39.0 2.2 %copy-start.1 = (f32[16,256,256]{2,1,0:T(8,128)S(1)}, f32[16,256,256]{2,1,0:T(8,128)}, u32[]{:S(2)}) copy-start(f32[16,256,256]{2,1,0:T(8,128)} %copy-done) | copy-start | bytes 12582916
  52.4 4.9 %collective-permute-start.5 = (bf16[256,2048]{1,0:T(8,128)(2,1)}, bf16[256,2048]{1,0:T(8,128)(2,1)S(1)}, u32[]{:S(2)}, u32[]{:S(2)}) collective-permute-start(bf16[256,2048]{1,0:T(8,128)(2,1)} %get-tuple-element.24), channel_id=1, source_target_pairs={{0,8},{8,0},{16,24},{24,16},{1,9},{9,1},{17,25},{25,17},{2,10},{10... | collective-permute-start | bytes 3145736 | tf_op jit(solution)/shard_map/ppermute | solution.py:226
  62.5 6.8 %collective-permute-start.6 = (bf16[256,2048]{1,0:T(8,128)(2,1)S(1)}, bf16[256,2048]{1,0:T(8,128)(2,1)S(1)}, u32[]{:S(2)}, u32[]{:S(2)}) collective-permute-start(bf16[256,2048]{1,0:T(8,128)(2,1)S(1)} %project.4), channel_id=1, source_target_pairs={{0,8},{8,0},{16,24},{24,16},{1,9},{9,1},{17,25},{25,17},{2,10},{10... | collective-permute-start | bytes 3145736 | tf_op jit(solution)/shard_map/ppermute | solution.py:226
  63.1 25.1 %collective-permute-start.7 = (bf16[256,2048]{1,0:T(8,128)(2,1)S(1)}, bf16[256,2048]{1,0:T(8,128)(2,1)S(1)}, u32[]{:S(2)}, u32[]{:S(2)}) collective-permute-start(bf16[256,2048]{1,0:T(8,128)(2,1)S(1)} %add_convert_fusion.2), channel_id=1, source_target_pairs={{0,16},{8,24},{16,0},{24,8},{1,17},{9,25},{17,1},{25,9},{2,18},{10... | collective-permute-start | bytes 3145736 | tf_op jit(solution)/shard_map/ppermute | solution.py:226

commit v3 on v2

--- a/solution.py
+++ b/solution.py
@@ -24,8 +24,9 @@
     if last:
         which_ref, weight_ref, refs = refs[0], refs[1], refs[2:]
     out_ref, refs = refs[0], refs[1:]
-    if last:
-        part_ref, refs = refs[0], refs[1:]
+    part_ref, refs = refs[0], refs[1:]
+    if not last:
+        part_ref[...] = docs_ref[...]
     bias, key_t, value_x = refs[:3]
     rows = query_ref.shape[0]
     span = kv_refs[0].shape[0] - DOC_ROWS
@@ -43,7 +44,7 @@
     for n, kv in enumerate(kv_refs):
         key_docs = kv[span:span + DOC_ROWS, :span].astype(jnp.float32)[:1]
         same = query_docs == key_docs
-        if causal:
+        if causal and n == 0:
             row = lax.broadcasted_iota(jnp.int32, (rows, span), 0)
             col = lax.broadcasted_iota(jnp.int32, (rows, span), 1)
             same = same & (col <= row)
@@ -103,8 +104,10 @@
         args, specs = args + [before], specs + [whole]
     flops = 6 * heads * rows * keys * HD
     if last is None:
-        outs = jax.ShapeDtypeStruct((heads, rows, 2 * HD), jnp.float32)
-        out_specs = whole
+        outs = (
+            jax.ShapeDtypeStruct((heads, rows, 2 * HD), jnp.float32),
+            jax.ShapeDtypeStruct(docs.shape, docs.dtype),
+        )
     else:
         which, weight, columns = last
         args = args + [which, weight]
@@ -113,7 +116,6 @@
             jax.ShapeDtypeStruct(query.shape, jnp.bfloat16),
             jax.ShapeDtypeStruct((rows, columns), jnp.bfloat16),
         )
-        out_specs = (whole, whole)
         scratch += [pltpu.VMEM((weight.shape[0], columns), jnp.bfloat16), pltpu.SemaphoreType.DMA]
         flops += 2 * rows * query.shape[1] * columns
     return pl.pallas_call(
@@ -122,9 +124,9 @@
         ),
         out_shape=outs,
         in_specs=specs,
-        out_specs=out_specs,
+        out_specs=(whole, whole),
         scratch_shapes=scratch,
-        compiler_params=pltpu.CompilerParams(vmem_limit_bytes=44 * 2**20),
+        compiler_params=pltpu.CompilerParams(vmem_limit_bytes=(16 if last is None else 28) * 2**20),
         cost_estimate=pl.CostEstimate(
             flops=flops,
             bytes_accessed=4 * query.size + blocks * 2 * kvs[0].size,
@@ -158,7 +160,7 @@
         ),
         compiler_params=pltpu.CompilerParams(vmem_limit_bytes=24 * 2**20),
         cost_estimate=pl.CostEstimate(
-            flops=2 * rows * depth * width,
+            flops=rows * depth * width // 4,
             bytes_accessed=2 * (depth * width + rows * width + rows * depth),
             transcendentals=0,
         ),
@@ -199,16 +201,16 @@
         odd = lax.axis_index("context") % 2 == 1
         two = up(own, 2)
         below = lax.ppermute(own, "context", [(i, i + 1) for i in range(0, n_context, 2)])
-        state = attend(query_rows, query_docs, [own], kv_count, causal=True)
-        two, below, state = lax.optimization_barrier((two, below, state))
+        two, below = lax.optimization_barrier((two, below))
         four = up(two, 2)
         beside = lax.ppermute(two, "context", [(i, i ^ 1) for i in range(n_context)])
-        state = attend(query_rows, query_docs, [two], kv_count, before=state)
-        four, beside, state = lax.optimization_barrier((four, beside, state))
+        state, query_docs = attend(query_rows, query_docs, [own, two], kv_count, causal=True)
+        four, beside, query_docs = lax.optimization_barrier((four, beside, query_docs))
         above = lax.ppermute(four, "context", [(i + 1, i) for i in range(0, n_context, 2)])
-        kvs = [beside, four, jnp.where(odd, below, above)]
+        state, query_docs = attend(query_rows, query_docs, [beside, four], kv_count, before=state)
+        kvs = [jnp.where(odd, below, above)]
     else:
-        state = attend(query_rows, query_docs, [own], kv_count, causal=True)
+        state, query_docs = attend(query_rows, query_docs, [own], kv_count, causal=True)
         kvs = [up(own, by) for by in range(1, min(back, n_context - 1) + 1)]
     attended, first_part = attend(
         query_rows, query_docs, kvs, kv_count, before=state, last=last

time: 90 us -> 88 us (0.978)
  waiting for transfers between devices: 27.6 us -> 24.4 us
  Pallas kernels: 34.8 us -> 36 us
    ppermute x1, waiting for transfers between devices: 7.1 us -> 0.01 us  [body(): lax.ppermute(four, 'context', [(i + 1, i) for i in range(0, n_context, 2)])]
    ppermute x2, waiting for transfers between devices: 0.01 us -> 2.46 us  [up(): return lax.ppermute(x, 'context', pairs)]
    ppermute x1, waiting for transfers between devices: 1.66 us -> 3.14 us  [body(): lax.ppermute(own, 'context', [(i, i + 1) for i in range(0, n_context, 2)])]
    pallas_call x3, Pallas kernels: 20.5 us -> 21.6 us  [attend(): pl.pallas_call(functools.partial(attend_kernel, kv_count, per_kv, blocks,...]
  transfers between devices with their start and end apart: 8 -> 8, of which waited for: 3 -> 3; matrix products, arithmetic and copies ran while one was open for 0% -> 0% of each run, Pallas kernels for 21% -> 24%
where the time goes in v3:
time: 88 us; the launch traced here: 87.7 us
  Pallas kernels  36 us (41%)
  waiting for transfers between devices  24.4 us (28%)
  starting transfers between devices  18 us (20%)
  local copies, waits for them, and re-layouts  6.45 us (7%)
  other arithmetic  2.64 us (3%)
    pallas_call x3, Pallas kernels, attend(): pl.pallas_call(functools.partial(attend_kernel, kv_count, per_kv, blocks,...  21.6 us
    ppermute x3, waiting for transfers between devices, reduced(): got = lax.ppermute(sent, 'tensor', [(i, i ^ step) for i in range(n_tensor)])  18.8 us
    pallas_call x3, Pallas kernels, project(): pl.pallas_call(project_kernel, out_shape=jax.ShapeDtypeStruct((rows, widt...  14.4 us
    ppermute x2, starting transfers between devices, up(): return lax.ppermute(x, 'context', pairs)  8.45 us
    unnamed x8, local copies, waits for them, and re-layouts  5.37 us
    ppermute x1, starting transfers between devices, body(): lax.ppermute(own, 'context', [(i, i + 1) for i in range(0, n_context, 2)])  3.41 us
    ppermute x1, waiting for transfers between devices, body(): lax.ppermute(own, 'context', [(i, i + 1) for i in range(0, n_context, 2)])  3.14 us
    ppermute x1, starting transfers between devices, body(): lax.ppermute(two, 'context', [(i, i ^ 1) for i in range(n_context)])  2.55 us
  transfers between devices with their start and end apart: 8, of which 3 were waited for; matrix products, arithmetic and copies ran while one was open for 0% of the time, Pallas kernels for 24%

profile of v3, /device:TPU:0, one launch (start us, length us, event | category | flops | bytes accessed | tf_op | source)
XLA Modules:
  0.0 87.7 jit_solution(8041820392464994023)
XLA Ops:
  0.0 0.7 add_convert_fusion.3
  0.7 1.0 %constant_dynamic-slice_fusion = (bf16[256,256]{1,0:T(8,128)(2,1)S(1)}, bf16[256,256]{1,0:T(8,128)(2,1)S(1)}) fusion(bf16[256,1024]{1,0:T(8,128)(2,1)} %param.7, s32[]{:T(128)S(6)} %select_n.24, bf16[256,1024]{1,0:T(8,128)(2,1)} %param.6), kind=kLoop, calls=%fused_computation.6 | loop fusion | bytes 524292 | tf_op jit(solution)/shard_map/dynamic_slice | solution.py:179
  1.7 5.0 %collective-permute-start = (bf16[272,512]{1,0:T(8,128)(2,1)S(1)}, bf16[272,512]{1,0:T(8,128)(2,1)S(1)}, u32[]{:S(2)}, u32[]{:S(2)}) collective-permute-start(bf16[272,512]{1,0:T(8,128)(2,1)S(1)} %pad_maximum_fusion.refs_0_), channel_id=1, source_target_pairs={{0,2},{1,3},{2,4},{3,5},{4,6},{5,7},{8,10},{9,11},{10,12},{11,13},... | collective-permute-start | bytes 835592 | tf_op jit(solution)/shard_map/ppermute | solution.py:190
  6.7 3.4 %collective-permute-start.1 = (bf16[272,512]{1,0:T(8,128)(2,1)S(1)}, bf16[272,512]{1,0:T(8,128)(2,1)S(1)}, u32[]{:S(2)}, u32[]{:S(2)}) collective-permute-start(bf16[272,512]{1,0:T(8,128)(2,1)S(1)} %pad_maximum_fusion.refs_0_), channel_id=1, source_target_pairs={{0,1},{2,3},{4,5},{6,7},{8,9},{10,11},{12,13},{14,15},{16,17},{18,... | collective-permute-start | bytes 835592 | tf_op jit(solution)/shard_map/ppermute | solution.py:203
  10.1 2.5 %collective-permute-done.refs_1_ = bf16[272,512]{1,0:T(8,128)(2,1)S(1)} collective-permute-done((bf16[272,512]{1,0:T(8,128)(2,1)S(1)}, bf16[272,512]{1,0:T(8,128)(2,1)S(1)}, u32[]{:S(2)}, u32[]{:S(2)}) %collective-permute-start) | collective-permute-done | bytes 278560 | tf_op jit(solution)/shard_map/ppermute | solution.py:190
  12.6 3.1 %collective-permute-done.1 = bf16[272,512]{1,0:T(8,128)(2,1)S(1)} collective-permute-done((bf16[272,512]{1,0:T(8,128)(2,1)S(1)}, bf16[272,512]{1,0:T(8,128)(2,1)S(1)}, u32[]{:S(2)}, u32[]{:S(2)}) %collective-permute-start.1) | collective-permute-done | bytes 278560 | tf_op jit(solution)/shard_map/ppermute | solution.py:203
  15.7 3.5 %collective-permute-start.2 = (bf16[272,512]{1,0:T(8,128)(2,1)S(1)}, bf16[272,512]{1,0:T(8,128)(2,1)S(1)}, u32[]{:S(2)}, u32[]{:S(2)}) collective-permute-start(bf16[272,512]{1,0:T(8,128)(2,1)S(1)} %collective-permute-done.refs_1_), channel_id=1, source_target_pairs={{0,2},{1,3},{2,4},{3,5},{4,6},{5,7},{8,10},{9,11},{10,12},{11,13},... | collective-permute-start | bytes 835592 | tf_op jit(solution)/shard_map/ppermute | solution.py:190
  19.2 2.5 %collective-permute-start.3 = (bf16[272,512]{1,0:T(8,128)(2,1)S(1)}, bf16[272,512]{1,0:T(8,128)(2,1)S(1)}, u32[]{:S(2)}, u32[]{:S(2)}) collective-permute-start(bf16[272,512]{1,0:T(8,128)(2,1)S(1)} %collective-permute-done.refs_1_), channel_id=1, source_target_pairs={{0,1},{1,0},{2,3},{3,2},{4,5},{5,4},{6,7},{7,6},{8,9},{9,8},{10,11... | collective-permute-start | bytes 835592 | tf_op jit(solution)/shard_map/ppermute | solution.py:206
  21.8 0.1 broadcast_in_dim.5.docs_ref
  21.8 0.0 copy-start
  21.9 1.2 %copy-done = bf16[256,2048]{1,0:T(8,128)(2,1)S(1)} copy-done((bf16[256,2048]{1,0:T(8,128)(2,1)S(1)}, bf16[256,2048]{1,0:T(8,128)(2,1)}, u32[]{:S(2)}) %copy-start) | copy-done | bytes 1048600
  23.1 0.0 copy-start.1
  23.1 4.8 %attend.3 = (f32[16,256,256]{2,1,0:T(8,128)S(1)}, f32[256,128]{1,0:T(8,128)S(1)}) custom-call(bf16[256,2048]{1,0:T(8,128)(2,1)S(1)} %copy-done, f32[256,128]{1,0:T(8,128)S(1)} %broadcast_in_dim.5.docs_ref, bf16[272,512]{1,0:T(8,128)(2,1)S(1)} %pad_maximum_fusion.refs_0_, bf16[272,512]{1,0:T(8,128)(2,1)S(1)} %collective-permute-done.refs_1_), custom_call_target="tpu_custom_call" | custom-call | flops 1610612736 | bytes 2654208 | tf_op jit(solution)/shard_map/attend/pallas_call | solution.py:121
  27.9 0.0 copy-start.2
  27.9 2.0 %copy-done.2 = f32[16,256,256]{2,1,0:T(8,128)} copy-done((f32[16,256,256]{2,1,0:T(8,128)}, f32[16,256,256]{2,1,0:T(8,128)S(1)}, u32[]{:S(2)}) %copy-start.2) | copy-done | bytes 4194328
  29.8 0.0 collective-permute-done.2.refs_1_
  29.9 0.0 collective-permute-done.3.refs_0_
  29.9 1.5 %collective-permute-start.4 = (bf16[272,512]{1,0:T(8,128)(2,1)S(1)}, bf16[272,512]{1,0:T(8,128)(2,1)S(1)}, u32[]{:S(2)}, u32[]{:S(2)}) collective-permute-start(bf16[272,512]{1,0:T(8,128)(2,1)S(1)} %collective-permute-done.2.refs_1_), channel_id=1, source_target_pairs={{1,0},{3,2},{5,4},{7,6},{9,8},{11,10},{13,12},{15,14},{17,16},{19,... | collective-permute-start | bytes 835592 | tf_op jit(solution)/shard_map/ppermute | solution.py:209
  31.3 0.0 copy-done.1
  31.3 0.0 copy-start.3
  31.4 2.2 %copy-done.3 = f32[16,256,256]{2,1,0:T(8,128)S(1)} copy-done((f32[16,256,256]{2,1,0:T(8,128)S(1)}, f32[16,256,256]{2,1,0:T(8,128)}, u32[]{:S(2)}) %copy-start.3) | copy-done | bytes 4194328
  33.5 6.7 %attend.4 = (f32[16,256,256]{2,1,0:T(8,128)S(1)}, f32[256,128]{1,0:T(8,128)S(1)}) custom-call(bf16[256,2048]{1,0:T(8,128)(2,1)S(1)} %copy-done.1, f32[256,128]{1,0:T(8,128)S(1)} %get-tuple-element.22.docs_ref, bf16[272,512]{1,0:T(8,128)(2,1)S(1)} %collective-permute-done.3.refs_0_, bf16[272,512]{1,0:T(8,128)(2,1)S(1)} %collective-permute-done.2.refs_1_, ...), custom_call_target="tpu_custom_call" | custom-call | flops 1610612736 | bytes 2654208 | tf_op jit(solution)/shard_map/attend/pallas_call | solution.py:121
  40.3 0.0 collective-permute-done.4
  40.3 10.1 %attend.5 = (bf16[256,2048]{1,0:T(8,128)(2,1)S(1)}, bf16[256,2048]{1,0:T(8,128)(2,1)S(1)}) custom-call(bf16[256,2048]{1,0:T(8,128)(2,1)S(1)} %copy-done.1, f32[256,128]{1,0:T(8,128)S(1)} %get-tuple-element.26.docs_ref, bf16[272,512]{1,0:T(8,128)(2,1)S(1)} %broadcast_select_fusion.refs_0_, f32[16,256,256]{2,1,0:T(8,128)S(1)} %get-tuple-element.28.refs_1_, ...), custom_call_target="tpu_custom_call" | custom-call | flops 2952790016 | bytes 2375680 | tf_op jit(solution)/shard_map/attend/pallas_call | solution.py:121
  50.4 0.1 collective-permute-start.5
  50.5 4.8 %project.3 = bf16[256,2048]{1,0:T(8,128)(2,1)S(1)} custom-call(s32[1]{0:T(128)} %bitcast.2.which_ref, bf16[256,2048]{1,0:T(8,128)(2,1)S(1)} %get-tuple-element.32.left_ref, bf16[2048,8192]{1,0:T(8,128)(2,1)} %weight_ref.5), custom_call_target="tpu_custom_call" | custom-call | flops 268435456 | bytes 10485760 | tf_op jit(solution)/shard_map/project/pallas_call | solution.py:149
  55.3 0.0 collective-permute-done.5
  55.3 0.4 add_convert_fusion.2
  55.7 4.8 %project.4 = bf16[256,2048]{1,0:T(8,128)(2,1)S(1)} custom-call(s32[1]{0:T(128)} %bitcast.3.which_ref, bf16[256,2048]{1,0:T(8,128)(2,1)S(1)} %get-tuple-element.32.left_ref, bf16[2048,8192]{1,0:T(8,128)(2,1)} %weight_ref.5), custom_call_target="tpu_custom_call" | custom-call | flops 268435456 | bytes 10485760 | tf_op jit(solution)/shard_map/project/pallas_call | solution.py:149
  60.5 0.5 collective-permute-start.6
  61.1 1.5 %collective-permute-start.7 = (bf16[256,2048]{1,0:T(8,128)(2,1)S(1)}, bf16[256,2048]{1,0:T(8,128)(2,1)S(1)}, u32[]{:S(2)}, u32[]{:S(2)}) collective-permute-start(bf16[256,2048]{1,0:T(8,128)(2,1)S(1)} %add_convert_fusion.2), channel_id=1, source_target_pairs={{0,16},{8,24},{16,0},{24,8},{1,17},{9,25},{17,1},{25,9},{2,18},{10... | collective-permute-start | bytes 3145736 | tf_op jit(solution)/shard_map/ppermute | solution.py:228
  62.6 4.8 %project.5 = bf16[256,2048]{1,0:T(8,128)(2,1)S(1)} custom-call(s32[1]{0:T(128)} %bitcast.which_ref, bf16[256,2048]{1,0:T(8,128)(2,1)S(1)} %get-tuple-element.32.left_ref, bf16[2048,8192]{1,0:T(8,128)(2,1)} %weight_ref.5), custom_call_target="tpu_custom_call" | custom-call | flops 268435456 | bytes 10485760 | tf_op jit(solution)/shard_map/project/pallas_call | solution.py:149
  67.4 0.0 collective-permute-done.6
  67.4 18.8 %collective-permute-done.7 = bf16[256,2048]{1,0:T(8,128)(2,1)S(1)} collective-permute-done((bf16[256,2048]{1,0:T(8,128)(2,1)S(1)}, bf16[256,2048]{1,0:T(8,128)(2,1)S(1)}, u32[]{:S(2)}, u32[]{:S(2)}) %collective-permute-start.7) | collective-permute-done | bytes 1048608 | tf_op jit(solution)/shard_map/ppermute | solution.py:228
  86.2 1.5 %add_convert_fusion = bf16[256,2048]{1,0:T(8,128)(2,1)} fusion(bf16[256,2048]{1,0:T(8,128)(2,1)S(1)} %collective-permute-done.7, bf16[256,2048]{1,0:T(8,128)(2,1)S(1)} %collective-permute-done.6, bf16[256,2048]{1,0:T(8,128)(2,1)S(1)} %project.5), kind=kLoop, calls=%fused_computation | loop fusion | flops 4194304 | bytes 4194304 | tf_op jit(solution)/shard_map/convert_element_type | solution.py:230
  (4 shorter events, 0.1 us)
Async XLA Ops:
  1.7 10.9 %collective-permute-start = (bf16[272,512]{1,0:T(8,128)(2,1)S(1)}, bf16[272,512]{1,0:T(8,128)(2,1)S(1)}, u32[]{:S(2)}, u32[]{:S(2)}) collective-permute-start(bf16[272,512]{1,0:T(8,128)(2,1)S(1)} %pad_maximum_fusion.refs_0_), channel_id=1, source_target_pairs={{0,2},{1,3},{2,4},{3,5},{4,6},{5,7},{8,10},{9,11},{10,12},{11,13},... | collective-permute-start | bytes 835592 | tf_op jit(solution)/shard_map/ppermute | solution.py:190
  6.7 9.0 %collective-permute-start.1 = (bf16[272,512]{1,0:T(8,128)(2,1)S(1)}, bf16[272,512]{1,0:T(8,128)(2,1)S(1)}, u32[]{:S(2)}, u32[]{:S(2)}) collective-permute-start(bf16[272,512]{1,0:T(8,128)(2,1)S(1)} %pad_maximum_fusion.refs_0_), channel_id=1, source_target_pairs={{0,1},{2,3},{4,5},{6,7},{8,9},{10,11},{12,13},{14,15},{16,17},{18,... | collective-permute-start | bytes 835592 | tf_op jit(solution)/shard_map/ppermute | solution.py:203
  15.7 14.1 %collective-permute-start.2 = (bf16[272,512]{1,0:T(8,128)(2,1)S(1)}, bf16[272,512]{1,0:T(8,128)(2,1)S(1)}, u32[]{:S(2)}, u32[]{:S(2)}) collective-permute-start(bf16[272,512]{1,0:T(8,128)(2,1)S(1)} %collective-permute-done.refs_1_), channel_id=1, source_target_pairs={{0,2},{1,3},{2,4},{3,5},{4,6},{5,7},{8,10},{9,11},{10,12},{11,13},... | collective-permute-start | bytes 835592 | tf_op jit(solution)/shard_map/ppermute | solution.py:190
  19.2 10.6 %collective-permute-start.3 = (bf16[272,512]{1,0:T(8,128)(2,1)S(1)}, bf16[272,512]{1,0:T(8,128)(2,1)S(1)}, u32[]{:S(2)}, u32[]{:S(2)}) collective-permute-start(bf16[272,512]{1,0:T(8,128)(2,1)S(1)} %collective-permute-done.refs_1_), channel_id=1, source_target_pairs={{0,1},{1,0},{2,3},{3,2},{4,5},{5,4},{6,7},{7,6},{8,9},{9,8},{10,11... | collective-permute-start | bytes 835592 | tf_op jit(solution)/shard_map/ppermute | solution.py:206
  21.8 1.2 %copy-start = (bf16[256,2048]{1,0:T(8,128)(2,1)S(1)}, bf16[256,2048]{1,0:T(8,128)(2,1)}, u32[]{:S(2)}) copy-start(bf16[256,2048]{1,0:T(8,128)(2,1)} %query_ref.5) | copy-start | bytes 3145732
  23.1 8.3 %copy-start.1 = (bf16[256,2048]{1,0:T(8,128)(2,1)S(1)}, bf16[256,2048]{1,0:T(8,128)(2,1)}, u32[]{:S(2)}) copy-start(bf16[256,2048]{1,0:T(8,128)(2,1)} %query_ref.5) | copy-start | bytes 3145732
  27.9 2.0 %copy-start.2 = (f32[16,256,256]{2,1,0:T(8,128)}, f32[16,256,256]{2,1,0:T(8,128)S(1)}, u32[]{:S(2)}) copy-start(f32[16,256,256]{2,1,0:T(8,128)S(1)} %get-tuple-element.25.refs_2_) | copy-start | bytes 12582916
  29.9 10.4 %collective-permute-start.4 = (bf16[272,512]{1,0:T(8,128)(2,1)S(1)}, bf16[272,512]{1,0:T(8,128)(2,1)S(1)}, u32[]{:S(2)}, u32[]{:S(2)}) collective-permute-start(bf16[272,512]{1,0:T(8,128)(2,1)S(1)} %collective-permute-done.2.refs_1_), channel_id=1, source_target_pairs={{1,0},{3,2},{5,4},{7,6},{9,8},{11,10},{13,12},{15,14},{17,16},{19,... | collective-permute-start | bytes 835592 | tf_op jit(solution)/shard_map/ppermute | solution.py:209
  31.3 2.2 %copy-start.3 = (f32[16,256,256]{2,1,0:T(8,128)S(1)}, f32[16,256,256]{2,1,0:T(8,128)}, u32[]{:S(2)}) copy-start(f32[16,256,256]{2,1,0:T(8,128)} %copy-done.2) | copy-start | bytes 12582916
  50.4 4.9 %collective-permute-start.5 = (bf16[256,2048]{1,0:T(8,128)(2,1)S(1)}, bf16[256,2048]{1,0:T(8,128)(2,1)S(1)}, u32[]{:S(2)}, u32[]{:S(2)}) collective-permute-start(bf16[256,2048]{1,0:T(8,128)(2,1)S(1)} %get-tuple-element.30), channel_id=1, source_target_pairs={{0,8},{8,0},{16,24},{24,16},{1,9},{9,1},{17,25},{25,17},{2,10},{10... | collective-permute-start | bytes 3145736 | tf_op jit(solution)/shard_map/ppermute | solution.py:228
  60.5 6.8 %collective-permute-start.6 = (bf16[256,2048]{1,0:T(8,128)(2,1)S(1)}, bf16[256,2048]{1,0:T(8,128)(2,1)S(1)}, u32[]{:S(2)}, u32[]{:S(2)}) collective-permute-start(bf16[256,2048]{1,0:T(8,128)(2,1)S(1)} %project.4), channel_id=1, source_target_pairs={{0,8},{8,0},{16,24},{24,16},{1,9},{9,1},{17,25},{25,17},{2,10},{10... | collective-permute-start | bytes 3145736 | tf_op jit(solution)/shard_map/ppermute | solution.py:228
  61.1 25.1 %collective-permute-start.7 = (bf16[256,2048]{1,0:T(8,128)(2,1)S(1)}, bf16[256,2048]{1,0:T(8,128)(2,1)S(1)}, u32[]{:S(2)}, u32[]{:S(2)}) collective-permute-start(bf16[256,2048]{1,0:T(8,128)(2,1)S(1)} %add_convert_fusion.2), channel_id=1, source_target_pairs={{0,16},{8,24},{16,0},{24,8},{1,17},{9,25},{17,1},{25,9},{2,18},{10... | collective-permute-start | bytes 3145736 | tf_op jit(solution)/shard_map/ppermute | solution.py:228
